TPU v7x, 32 devices: a whole 2x2x4 slice. The times are simulated.
32 devices in a mesh: row: 4 (over x, core), col: 8 (over z, y).
Axes of the slice: x: 2, y: 2, z: 4, core: 2. Of those that a mesh axis runs over, the one named last changes fastest.
Arguments:
- edge_h: int32 [128, 1024], P('row', 'col'), may hold values from 0 to 7
- edge_v: int32 [128, 1024], P('row', 'col'), may hold values from 0 to 7
- pads: int32 [128, 1024], P('row', 'col'), may hold values 0 or 1
- loads: int32 [256, 128, 1024], P(None, 'row', 'col'), may hold values from 0 to 7
- scales: float32 [256, 8], replicated, may hold values from 0.25 to 4
Outputs:
- drop: float32 [256, 128, 1024], P(None, 'row', 'col')
- res_norms: float32 [256, 5], replicated
All inputs are finite; a program needn't handle non-finite values. No bound on the sum of `pads` on one device may be relied on, other than what follows from the above.
Results may differ from a plain program's by a relative error of at most 0.0003.
Values sent between devices are 32-bit elements; how exact they have to be, the bound alone decides.
A program may use at most 128 MiB of HBM per device.

v0:
```python
import functools

import jax
import jax.numpy as jnp
from jax import lax
from jax.experimental import pallas as pl
from jax.experimental.pallas import tpu as pltpu
from jax.sharding import PartitionSpec as P

ITERS = 4
H = ITERS
LANES = 128
MESH = pl.DeviceIdType.MESH

edge_table = (0.5, 0.8, 1.2, 1.7, 2.3, 3.0, 3.8, 4.7)
load_table = (0.25, 0.5, 1.0, 1.5, 2.0, 3.0, 4.0, 6.0)
pad_conductance = 20.0
leakage = 0.05

DIRS = [(-1, 0), (1, 0), (0, -1), (0, 1), (-1, -1), (-1, 1), (1, -1), (1, 1)]
MOMENTS = [(m // 2, m - m // 2) for m in range(2 * ITERS)]
GRAM = [(i, j) for i in range(ITERS + 1) for j in range(i, ITERS + 1)]
SUMS = len(MOMENTS) + len(GRAM)
SLOTS = -(-SUMS // 8) * 8


def lookup_edge(classes):
    total = jnp.zeros(classes.shape, jnp.float32)
    for number, amount in enumerate(edge_table):
        total = jnp.where(classes == number, jnp.float32(amount), total)
    return total


def pick(classes, rows):
    low = (classes & 1) == 0
    mid = (classes & 2) == 0
    high = (classes & 4) == 0
    a = [jnp.where(low, rows[2 * i], rows[2 * i + 1]) for i in range(4)]
    b = [jnp.where(mid, a[0], a[1]), jnp.where(mid, a[2], a[3])]
    return jnp.where(high, b[0], b[1])


def kernel(
    nr, nc, maps, loads, weights, drop, norms,
    rowbuf, colbuf, corner, mrow, mcol, mcorner,
    z, gE, gW, gS, gN, diag, recip, acc, part, slots_row, mid, slots_col, coef,
    send_sem, recv_sem, send_row, recv_row, send_col, recv_col,
):
    halves, rows, cols, _ = loads.shape
    ext_r, ext_c = rows + 2 * H, cols + 8
    me_r, me_c = lax.axis_index("row"), lax.axis_index("col")

    def exists(dr, dc):
        r, c = me_r + dr, me_c + dc
        return (r >= 0) & (r < nr) & (c >= 0) & (c < nc)

    def side(d):
        return 0 if d < 0 else 1

    def load_copy(k):
        dr, dc = DIRS[k]
        rs = pl.ds(0, H) if dr < 0 else pl.ds(rows - H, H)
        cs = pl.ds(0, 8) if dc < 0 else pl.ds(cols - 8, 8)
        if dc == 0:
            src, dst = loads.at[:, rs], rowbuf.at[side(-dr)]
        elif dr == 0:
            src, dst = loads.at[:, :, cs], colbuf.at[side(-dc)]
        else:
            src, dst = loads.at[:, rs, cs], corner.at[2 * side(-dr) + side(-dc)]
        return pltpu.make_async_remote_copy(
            src_ref=src, dst_ref=dst, send_sem=send_sem.at[k], recv_sem=recv_sem.at[k],
            device_id=(me_r + dr, me_c + dc), device_id_type=MESH,
        )

    def map_copy(k):
        dr, dc = DIRS[k]
        rs = pl.ds(0, 8) if dr < 0 else pl.ds(rows - 8, 8)
        if dc == 0:
            src, dst = maps.at[:, rs], mrow.at[side(-dr)]
        elif dr == 0:
            src, dst = maps, mcol.at[side(-dc)]
        else:
            src, dst = maps.at[:, rs], mcorner.at[2 * side(-dr) + side(-dc)]
        return pltpu.make_async_remote_copy(
            src_ref=src, dst_ref=dst, send_sem=send_sem.at[8 + k], recv_sem=recv_sem.at[8 + k],
            device_id=(me_r + dr, me_c + dc), device_id_type=MESH,
        )

    barrier = pltpu.get_barrier_semaphore()
    for j in range(1, nr):
        pl.semaphore_signal(
            barrier, inc=1, device_id=(lax.rem(me_r + j, nr), me_c), device_id_type=MESH
        )
    for j in range(1, nc):
        pl.semaphore_signal(
            barrier, inc=1, device_id=(me_r, lax.rem(me_c + j, nc)), device_id_type=MESH
        )
    for dr, dc in DIRS[4:]:
        corner_id = (lax.rem(me_r + dr + nr, nr), lax.rem(me_c + dc + nc, nc))
        pl.semaphore_signal(barrier, inc=1, device_id=corner_id, device_id_type=MESH)
    pl.semaphore_wait(barrier, nr + nc - 2 + 4)

    for k in range(8):

        @pl.when(exists(*DIRS[k]))
        def _():
            map_copy(k).start()

    for k in range(8):

        @pl.when(exists(*DIRS[k]))
        def _():
            load_copy(k).start()

    for k in range(8):

        @pl.when(exists(-DIRS[k][0], -DIRS[k][1]))
        def _():
            map_copy(k).wait_recv()

    pad_rows = jnp.zeros((LANES - ext_r - 1, cols), jnp.float32)

    def stretch(north, own, south):
        tall = jnp.concatenate([north[8 - H :], own, south[:H]], axis=0).astype(jnp.float32)
        before = north[7 - H : 8 - H].astype(jnp.float32)
        return jnp.concatenate([tall, pad_rows, before], axis=0).T

    sub8 = lax.broadcasted_iota(jnp.int32, (8, LANES), 0)

    def widened(m):
        own = stretch(mrow[0, m], maps[m], mrow[1, m])
        west = stretch(mcorner[0, m], mcol[0, m], mcorner[2, m])
        east = stretch(mcorner[1, m], mcol[1, m], mcorner[3, m])
        rim = jnp.where(sub8 < H, east[:8], west[cols - 8 :])
        return jnp.concatenate([own, rim], axis=0), west[cols - 8 :]

    sub = lax.broadcasted_iota(jnp.int32, (ext_c, LANES), 0)
    lane = lax.broadcasted_iota(jnp.int32, (ext_c, LANES), 1)
    col_id = me_c * cols + jnp.where(sub >= cols + H, sub - ext_c, sub)
    row_id = me_r * rows + jnp.where(lane == LANES - 1, -1, lane) - H
    east_class, west_class = widened(0)
    e = jnp.where((col_id >= 0) & (col_id < nc * cols - 1), lookup_edge(east_class), 0.0)
    s = jnp.where((row_id >= 0) & (row_id < nr * rows - 1), lookup_edge(widened(1)[0]), 0.0)
    w = pltpu.roll(e, 1, 0)
    beyond = jnp.where(me_c > 0, lookup_edge(west_class), 0.0)
    rim_w = jnp.where(sub8 < H, w[cols:], pltpu.roll(beyond, 1, 0))
    w = jnp.concatenate([w[:cols], rim_w], axis=0)
    n = pltpu.roll(s, 1, 1)
    d = e + w + s + n + jnp.where(widened(2)[0] == 1.0, pad_conductance, 0.0) + leakage
    inv = 1.0 / d
    inv = inv * (2.0 - d * inv)
    inv = inv * (2.0 - d * inv)
    for ref, value in (
        (gE, e * inv), (gW, w * inv), (gS, s * inv), (gN, n * inv), (diag, d), (recip, inv)
    ):
        for r in range(ext_r):
            ref[r] = jnp.broadcast_to(value[:, r : r + 1], (ext_c, LANES))

    wrows = [[weights[h, c : c + 1, :] for c in range(8)] for h in range(halves)]

    @pl.loop(0, rows)
    def _(r):
        for h in range(halves):
            z[0, h, r + H, :cols] = pick(loads[h, r], wrows[h]) * recip[r + H, :cols]

    for k in range(8):

        @pl.when(exists(-DIRS[k][0], -DIRS[k][1]))
        def _():
            load_copy(k).wait_recv()

    @pl.loop(0, rows)
    def _(r):
        for h in range(halves):
            rim = jnp.where(sub8 < H, colbuf[1, h, r], colbuf[0, h, r])
            z[0, h, r + H, cols:] = pick(rim, wrows[h]) * recip[r + H, cols:]

    @pl.loop(0, H)
    def _(i):
        for h in range(halves):
            for q, base in ((0, 0), (1, rows + H)):
                r = base + i
                z[0, h, r, :cols] = pick(rowbuf[q, h, i], wrows[h]) * recip[r, :cols]
                rim = jnp.where(sub8 < H, corner[2 * q + 1, h, i], corner[2 * q, h, i])
                z[0, h, r, cols:] = pick(rim, wrows[h]) * recip[r, cols:]

    for k in range(ITERS):

        @pl.loop(k + 1, ext_r - k - 1)
        def _(r):
            for h in range(halves):
                centre = z[k, h, r]
                z[k + 1, h, r] = (
                    gE[r] * pltpu.roll(centre, ext_c - 1, 0)
                    + gW[r] * pltpu.roll(centre, 1, 0)
                ) + (gS[r] * z[k, h, r + 1] + gN[r] * z[k, h, r - 1])

    acc[...] = jnp.zeros_like(acc)
    for h in range(halves):

        @pl.loop(H, rows + H)
        def _(r):
            totals = None
            for t in range(cols // 8):
                at = pl.ds(8 * t, 8)
                zs = [z[i, h, r, at] for i in range(ITERS + 1)]
                dd = diag[r, at]
                vs = [dd * x for x in zs]
                terms = [zs[i] * vs[j] for i, j in MOMENTS] + [vs[i] * vs[j] for i, j in GRAM]
                totals = terms if totals is None else [a + b for a, b in zip(totals, terms)]
            for i, total in enumerate(totals):
                acc[h, i] += total

    for h in range(halves):
        for i in range(SLOTS):
            part[h, i : i + 1] = jnp.sum(acc[h, i], axis=0, keepdims=True)

    def share(src, slots, me, count, axis, sends, recvs):
        def copy(j):
            other = lax.rem(me + j, count)
            target = (other, me_c) if axis == "row" else (me_r, other)
            return pltpu.make_async_remote_copy(
                src_ref=src, dst_ref=slots.at[me], send_sem=sends.at[j], recv_sem=recvs.at[j],
                device_id=target, device_id_type=MESH,
            )

        slots[me] = src[...]
        for j in range(1, count):
            copy(j).start()
        for j in range(1, count):
            copy(j).wait_recv()
        for j in range(1, count):
            copy(j).wait_send()
        total = slots[0]
        for i in range(1, count):
            total = total + slots[i]
        return total

    mid[...] = share(part, slots_row, me_r, nr, "row", send_row, recv_row)
    coef[...] = share(mid, slots_col, me_c, nc, "col", send_col, recv_col)

    def row_of(i):
        return coef[:, i, :]

    moment = [row_of(i) for i in range(len(MOMENTS))]
    gram = {pair: row_of(len(MOMENTS) + i) for i, pair in enumerate(GRAM)}
    zero = jnp.zeros_like(moment[0])
    one = jnp.ones_like(moment[0])

    def energy(a):
        total = None
        for i in range(len(a)):
            for j in range(len(a)):
                term = a[i] * a[j] * moment[i + j]
                total = term if total is None else total + term
        return total

    def stiffness(b):
        total = None
        for i in range(len(b)):
            for j in range(len(b)):
                term = b[i] * b[j] * (moment[i + j] - moment[i + j + 1])
                total = term if total is None else total + term
        return total

    def square(a):
        total = None
        for i in range(len(a)):
            for j in range(i, len(a)):
                term = a[i] * a[j] * gram[i, j]
                term = term if i == j else 2.0 * term
                total = term if total is None else total + term
        return jnp.sqrt(jnp.maximum(total, 0.0))

    resid, direction, answer = [one], [one], []
    gamma = moment[0]
    results = [square(resid)]
    for k in range(ITERS):
        alpha = gamma / stiffness(direction)
        answer = [
            (answer[i] if i < len(answer) else zero) + alpha * direction[i]
            for i in range(len(direction))
        ]
        image = [
            (direction[i] if i < len(direction) else zero)
            - (direction[i - 1] if i > 0 else zero)
            for i in range(len(direction) + 1)
        ]
        resid = [
            (resid[i] if i < len(resid) else zero) - alpha * image[i] for i in range(len(image))
        ]
        results.append(square(resid))
        if k + 1 < ITERS:
            gamma_new = energy(resid)
            ratio = gamma_new / gamma
            direction = [
                resid[i] + (ratio * direction[i] if i < len(direction) else zero)
                for i in range(len(resid))
            ]
            gamma = gamma_new
    for i, value in enumerate(results):
        norms[:, i, :] = value
    for i in range(ITERS + 1, norms.shape[1]):
        norms[:, i, :] = zero

    for h in range(halves):
        scale = [answer[i][h : h + 1] for i in range(ITERS)]

        @pl.loop(0, rows)
        def _(r):
            total = scale[0] * z[0, h, r + H, :cols]
            for i in range(1, ITERS):
                total = total + scale[i] * z[i, h, r + H, :cols]
            drop[h, r] = total

    for k in range(8):

        @pl.when(exists(*DIRS[k]))
        def _():
            map_copy(k).wait_send()
            load_copy(k).wait_send()


def local(nr, nc, edge_h, edge_v, pads, loads, scales):
    scen, rows, cols = loads.shape
    halves = scen // LANES
    weights = -scales * jnp.asarray(load_table, jnp.float32)[None, :]
    weights = weights.reshape(halves, LANES, 8).transpose(0, 2, 1)
    maps = jnp.stack([edge_h, edge_v, pads])
    turned = loads.reshape(halves, LANES, rows, cols).transpose(0, 2, 3, 1)
    ext_r, ext_c = rows + 2 * H, cols + 8
    f32, i32 = jnp.float32, jnp.int32
    norm_rows = -(-(ITERS + 1) // 8) * 8
    vmem = pl.BlockSpec(memory_space=pltpu.VMEM)
    dma = pltpu.SemaphoreType.DMA
    drop, norms = pl.pallas_call(
        functools.partial(kernel, nr, nc),
        out_shape=(
            jax.ShapeDtypeStruct((halves, rows, cols, LANES), f32),
            jax.ShapeDtypeStruct((halves, norm_rows, LANES), f32),
        ),
        in_specs=[vmem] * 3,
        out_specs=(vmem, vmem),
        scratch_shapes=[
            pltpu.VMEM((2, halves, H, cols, LANES), i32),
            pltpu.VMEM((2, halves, rows, 8, LANES), i32),
            pltpu.VMEM((4, halves, H, 8, LANES), i32),
            pltpu.VMEM((2, 3, 8, cols), i32),
            pltpu.VMEM((2, 3, rows, cols), i32),
            pltpu.VMEM((4, 3, 8, cols), i32),
            pltpu.VMEM((ITERS + 1, halves, ext_r, ext_c, LANES), f32),
            *[pltpu.VMEM((ext_r, ext_c, LANES), f32) for _ in range(6)],
            pltpu.VMEM((halves, SLOTS, 8, LANES), f32),
            pltpu.VMEM((halves, SLOTS, LANES), f32),
            pltpu.VMEM((nr, halves, SLOTS, LANES), f32),
            pltpu.VMEM((halves, SLOTS, LANES), f32),
            pltpu.VMEM((nc, halves, SLOTS, LANES), f32),
            pltpu.VMEM((halves, SLOTS, LANES), f32),
            dma((16,)),
            dma((16,)),
            dma((nr,)),
            dma((nr,)),
            dma((nc,)),
            dma((nc,)),
        ],
        compiler_params=pltpu.CompilerParams(
            collective_id=0, has_side_effects=True, vmem_limit_bytes=67043328
        ),
        name="grid_cg",
    )(maps, turned, weights)
    drop = drop.transpose(0, 3, 1, 2).reshape(scen, rows, cols)
    norms = norms.transpose(0, 2, 1).reshape(scen, norm_rows)[:, : ITERS + 1]
    return drop, norms


def solution(mesh):
    return jax.shard_map(
        functools.partial(local, mesh.shape["row"], mesh.shape["col"]),
        mesh=mesh,
        in_specs=(P("row", "col"), P("row", "col"), P("row", "col"), P(None, "row", "col"), P()),
        out_specs=(P(None, "row", "col"), P()),
        check_vma=False,
    )
```

profile of v0, /device:TPU:0, one launch (start us, length us, event | category | flops | bytes accessed | tf_op | source)
XLA Modules:
  0.0 70.4 jit_solution(8506819614391864484)
XLA Ops:
  0.6 1.4 %multiply_bitcast_fusion.weights = f32[2,8,128]{2,1,0:T(8,128)} fusion(f32[256,8]{0,1:T(8,128)} %param.10, f32[8]{0:T(128)} %constant.2.clone), kind=kLoop, calls=%fused_computation.1 | loop fusion | flops 4096 | bytes 16416 | tf_op jit(solution)/shard_map/transpose | solution.py:328
  2.0 1.4 %pad_add_fusion.maps = s32[3,32,128]{2,1,0:T(8,128)} fusion(s32[1,32,128]{2,1,0:T(8,128)} %bitcast.19, s32[1,32,128]{2,1,0:T(8,128)} %bitcast.20, s32[1,32,128]{2,1,0:T(8,128)} %bitcast.21), kind=kLoop, calls=%fused_computation | loop fusion | flops 24576 | bytes 98304 | tf_op jit(solution)/shard_map/stack | solution.py:329
  3.4 5.3 %copy.8 = s32[2,128,32,128]{1,3,2,0:T(8,128)} copy(s32[2,128,32,128]{3,2,1,0:T(8,128)} %bitcast.16) | data formatting | bytes 8388608 | tf_op jit(solution)/shard_map/reshape | solution.py:330
  8.7 55.7 %grid_cg.1 = (f32[2,32,128,128]{3,2,1,0:T(8,128)}, f32[2,8,128]{2,1,0:T(8,128)}) custom-call(s32[3,32,128]{2,1,0:T(8,128)} %pad_add_fusion.maps, s32[2,32,128,128]{3,2,1,0:T(8,128)} %bitcast.15, f32[2,8,128]{2,1,0:T(8,128)} %multiply_bitcast_fusion.weights), custom_call_target="tpu_custom_call" | custom-call | tf_op jit(solution)/shard_map/grid_cg/pallas_call | solution.py:336
  64.4 0.0 copy-start
  64.4 5.4 %copy.9 = f32[2,128,32,128]{3,2,1,0:T(8,128)} copy(f32[2,128,32,128]{1,3,2,0:T(8,128)} %bitcast.18) | data formatting | bytes 8388608 | tf_op jit(solution)/shard_map/transpose | solution.py:371
  69.8 0.0 copy-done
  69.8 0.6 copy.11
Async XLA Ops:
  64.4 5.5 %copy-start = (f32[2,8,128]{2,1,0:T(8,128)S(1)}, f32[2,8,128]{2,1,0:T(8,128)}, u32[]{:S(2)}) copy-start(f32[2,8,128]{2,1,0:T(8,128)} %get-tuple-element.5) | copy-start | bytes 24580
where the time goes:
time: 70.8 us; the launch traced here: 70.4 us
  Pallas kernels  55.7 us (79%)
  local copies, waits for them, and re-layouts  11.4 us (16%)
  other arithmetic  2.74 us (4%)
    pallas_call x1, Pallas kernels, local(): pl.pallas_call(functools.partial(kernel, nr, nc), out_shape=(jax.ShapeDty...  55.7 us
    transpose x1, local copies, waits for them, and re-layouts, local(): drop = drop.transpose(0, 3, 1, 2).reshape(scen, rows, cols)  5.44 us
    reshape x1, local copies, waits for them, and re-layouts, local(): turned = loads.reshape(halves, LANES, rows, cols).transpose(0, 2, 3, 1)  5.34 us

commit v1 on v0

--- a/solution.py
+++ b/solution.py
@@ -18,9 +18,16 @@
 leakage = 0.05
 
 DIRS = [(-1, 0), (1, 0), (0, -1), (0, 1), (-1, -1), (-1, 1), (1, -1), (1, 1)]
-MOMENTS = [(m // 2, m - m // 2) for m in range(2 * ITERS)]
-GRAM = [(i, j) for i in range(ITERS + 1) for j in range(i, ITERS + 1)]
-SUMS = len(MOMENTS) + len(GRAM)
+LAST = ITERS - 1
+MU = 0
+NU = 1
+EP = NU + ITERS
+KA = EP + 2 * ITERS - 2
+VV = KA + 2 * ITERS - 3
+VW = VV + 1
+WW = VW + ITERS
+PAIRS = [(i, j) for i in range(ITERS) for j in range(i, ITERS)]
+SUMS = WW + len(PAIRS)
 SLOTS = -(-SUMS // 8) * 8
 
 
@@ -205,8 +212,16 @@
                 at = pl.ds(8 * t, 8)
                 zs = [z[i, h, r, at] for i in range(ITERS + 1)]
                 dd = diag[r, at]
-                vs = [dd * x for x in zs]
-                terms = [zs[i] * vs[j] for i, j in MOMENTS] + [vs[i] * vs[j] for i, j in GRAM]
+                es = [zs[i] - zs[i + 1] for i in range(ITERS)]
+                fs = [es[i] - es[i + 1] for i in range(LAST)]
+                ws = [dd * e for e in es]
+                top = dd * zs[ITERS]
+                terms = [zs[LAST] * (dd * zs[LAST])]
+                terms += [zs[LAST] * ws[i] for i in range(ITERS)]
+                terms += [es[m // 2] * ws[m - m // 2] for m in range(2 * ITERS - 2)]
+                terms += [fs[m // 2] * ws[m - m // 2] for m in range(2 * ITERS - 3)]
+                terms += [top * top] + [top * ws[i] for i in range(ITERS)]
+                terms += [ws[i] * ws[j] for i, j in PAIRS]
                 totals = terms if totals is None else [a + b for a, b in zip(totals, terms)]
             for i, total in enumerate(totals):
                 acc[h, i] += total
@@ -242,61 +257,50 @@
     def row_of(i):
         return coef[:, i, :]
 
-    moment = [row_of(i) for i in range(len(MOMENTS))]
-    gram = {pair: row_of(len(MOMENTS) + i) for i, pair in enumerate(GRAM)}
-    zero = jnp.zeros_like(moment[0])
-    one = jnp.ones_like(moment[0])
-
-    def energy(a):
-        total = None
-        for i in range(len(a)):
-            for j in range(len(a)):
-                term = a[i] * a[j] * moment[i + j]
-                total = term if total is None else total + term
-        return total
-
-    def stiffness(b):
-        total = None
-        for i in range(len(b)):
-            for j in range(len(b)):
-                term = b[i] * b[j] * (moment[i + j] - moment[i + j + 1])
-                total = term if total is None else total + term
-        return total
-
-    def square(a):
+    zero = jnp.zeros_like(row_of(0))
+    one = jnp.ones_like(zero)
+    cross = {pair: row_of(WW + i) for i, pair in enumerate(PAIRS)}
+
+    def quadratic(a, entry):
         total = None
         for i in range(len(a)):
             for j in range(i, len(a)):
-                term = a[i] * a[j] * gram[i, j]
+                term = a[i] * a[j] * entry(i, j)
                 term = term if i == j else 2.0 * term
                 total = term if total is None else total + term
+        return total
+
+    def energy(c):
+        edge = sum(c[i] * row_of(NU + i) for i in range(LAST))
+        return row_of(MU) + 2.0 * edge + quadratic(c[:LAST], lambda i, j: row_of(EP + i + j))
+
+    def stiffness(s, b):
+        edge = sum(b[i] * row_of(EP + LAST + i) for i in range(LAST))
+        inner = quadratic(b, lambda i, j: row_of(KA + i + j))
+        return s * (s * row_of(NU + LAST) + 2.0 * edge) + inner
+
+    def norm(c):
+        edge = sum(c[i] * row_of(VW + i) for i in range(ITERS))
+        total = row_of(VV) + 2.0 * edge + quadratic(c, lambda i, j: cross[i, j])
         return jnp.sqrt(jnp.maximum(total, 0.0))
 
-    resid, direction, answer = [one], [one], []
-    gamma = moment[0]
-    results = [square(resid)]
+    c, s_top, b = [one] * ITERS, one, [one] * LAST
+    answer = [zero] * ITERS
+    gamma = energy(c)
+    results = [norm(c)]
     for k in range(ITERS):
-        alpha = gamma / stiffness(direction)
-        answer = [
-            (answer[i] if i < len(answer) else zero) + alpha * direction[i]
-            for i in range(len(direction))
-        ]
-        image = [
-            (direction[i] if i < len(direction) else zero)
-            - (direction[i - 1] if i > 0 else zero)
-            for i in range(len(direction) + 1)
-        ]
-        resid = [
-            (resid[i] if i < len(resid) else zero) - alpha * image[i] for i in range(len(image))
-        ]
-        results.append(square(resid))
+        alpha = gamma / stiffness(s_top, b)
+        ends = [zero] + b + [s_top]
+        for i in range(k + 1):
+            step = alpha * (ends[i + 1] - ends[i])
+            answer[i] = answer[i] + step
+            c[i] = c[i] - step
+        results.append(norm(c))
         if k + 1 < ITERS:
-            gamma_new = energy(resid)
+            gamma_new = energy(c)
             ratio = gamma_new / gamma
-            direction = [
-                resid[i] + (ratio * direction[i] if i < len(direction) else zero)
-                for i in range(len(resid))
-            ]
+            s_top = 1.0 + ratio * s_top
+            b = [c[i] + ratio * b[i] for i in range(LAST)]
             gamma = gamma_new
     for i, value in enumerate(results):
         norms[:, i, :] = value

time: 70.8 us -> 75.4 us (1.065)
  Pallas kernels: 55.7 us -> 60.2 us
    pallas_call x1, Pallas kernels: 55.7 us -> 60.2 us  [local(): pl.pallas_call(functools.partial(kernel, nr, nc), out_shape=(jax.ShapeDty...]
where the time goes in v1:
time: 75.4 us; the launch traced here: 75 us
  Pallas kernels  60.2 us (80%)
  local copies, waits for them, and re-layouts  11.4 us (15%)
  other arithmetic  2.74 us (4%)
    pallas_call x1, Pallas kernels, local(): pl.pallas_call(functools.partial(kernel, nr, nc), out_shape=(jax.ShapeDty...  60.2 us
    transpose x1, local copies, waits for them, and re-layouts, local(): drop = drop.transpose(0, 3, 1, 2).reshape(scen, rows, cols)  5.44 us
    reshape x1, local copies, waits for them, and re-layouts, local(): turned = loads.reshape(halves, LANES, rows, cols).transpose(0, 2, 3, 1)  5.34 us

profile of v1, /device:TPU:0, one launch (start us, length us, event | category | flops | bytes accessed | tf_op | source)
XLA Modules:
  0.0 75.0 jit_solution(17639996630495717353)
XLA Ops:
  0.6 1.4 %multiply_bitcast_fusion.weights = f32[2,8,128]{2,1,0:T(8,128)} fusion(f32[256,8]{0,1:T(8,128)} %param.10, f32[8]{0:T(128)} %constant.2.clone), kind=kLoop, calls=%fused_computation.1 | loop fusion | flops 4096 | bytes 16416 | tf_op jit(solution)/shard_map/transpose | solution.py:332
  2.0 1.4 %pad_add_fusion.maps = s32[3,32,128]{2,1,0:T(8,128)} fusion(s32[1,32,128]{2,1,0:T(8,128)} %bitcast.19, s32[1,32,128]{2,1,0:T(8,128)} %bitcast.20, s32[1,32,128]{2,1,0:T(8,128)} %bitcast.21), kind=kLoop, calls=%fused_computation | loop fusion | flops 24576 | bytes 98304 | tf_op jit(solution)/shard_map/stack | solution.py:333
  3.4 5.3 %copy.8 = s32[2,128,32,128]{1,3,2,0:T(8,128)} copy(s32[2,128,32,128]{3,2,1,0:T(8,128)} %bitcast.16) | data formatting | bytes 8388608 | tf_op jit(solution)/shard_map/reshape | solution.py:334
  8.7 60.2 %grid_cg.1 = (f32[2,32,128,128]{3,2,1,0:T(8,128)}, f32[2,8,128]{2,1,0:T(8,128)}) custom-call(s32[3,32,128]{2,1,0:T(8,128)} %pad_add_fusion.maps, s32[2,32,128,128]{3,2,1,0:T(8,128)} %bitcast.15, f32[2,8,128]{2,1,0:T(8,128)} %multiply_bitcast_fusion.weights), custom_call_target="tpu_custom_call" | custom-call | tf_op jit(solution)/shard_map/grid_cg/pallas_call | solution.py:340
  68.9 0.0 copy-start
  68.9 5.4 %copy.9 = f32[2,128,32,128]{3,2,1,0:T(8,128)} copy(f32[2,128,32,128]{1,3,2,0:T(8,128)} %bitcast.18) | data formatting | bytes 8388608 | tf_op jit(solution)/shard_map/transpose | solution.py:375
  74.4 0.0 copy-done
  74.4 0.6 copy.11
Async XLA Ops:
  68.9 5.5 %copy-start = (f32[2,8,128]{2,1,0:T(8,128)S(1)}, f32[2,8,128]{2,1,0:T(8,128)}, u32[]{:S(2)}) copy-start(f32[2,8,128]{2,1,0:T(8,128)} %get-tuple-element.5) | copy-start | bytes 24580
